TPU v7x, 32 devices: a whole 2x2x4 slice. The times are simulated.
32 devices in a mesh: dp: 1, vocab: 32 (over z, y, x, core).
Axes of the slice: x: 2, y: 2, z: 4, core: 2. Of those that a mesh axis runs over, the one named last changes fastest.
Arguments:
- input_ids: int32 [256], P('dp'), may hold values from 0 to 63999
- target_ids: int32 [256], P('dp'), may hold values from 0 to 63999
- loss_mask: int32 [256], P('dp'), may hold values 0 or 1
- final_hidden: bfloat16 [256, 3584], P('dp'), may hold values from -5 to 5, as said below
- norm_gain: float32 [3584], replicated, may hold values from 0.25 to 1.75
- embed_cotangent: bfloat16 [256, 3584], P('dp'), may hold values from -0.059814453 to 0.059814453
- table: bfloat16 [64000, 3584], P(('dp', 'vocab')), may hold values from -0.08351914 to 0.08351914, as said below
Outputs:
- embedded: bfloat16 [256, 3584], P('dp')
- loss: float32 [], replicated
- grad_hidden: bfloat16 [256, 3584], P('dp')
- gain_grad: float32 [3584], replicated
- table_grad: bfloat16 [64000, 3584], P(('dp', 'vocab'))
Inputs may be any that keep to these rules, and one draw needn't show every extreme that they name: Every entry of table lies within -5 / sqrt(3584) and 5 / sqrt(3584). Every entry of final_hidden lies within -5 and 5.
All inputs are finite; a program needn't handle non-finite values.
Results may differ from a plain program's by a relative error of at most 0.003.
Values may be sent and summed in bfloat16 or wider, within the bound.
A program may use at most 256 MiB of HBM per device.

v0:
```python
import math
import jax
import jax.numpy as jnp
from jax import lax
from jax.sharding import PartitionSpec as P

SOFTCAP = 30
EPSILON = 1e-06


def norm_backward(upstream, widened, inv_rms, norm_gain):
    scaled_up = upstream * norm_gain
    mean_dot = jnp.mean(scaled_up * widened, axis=1, keepdims=True)
    gradient = inv_rms * scaled_up - widened * (inv_rms * inv_rms * inv_rms) * mean_dot
    gain_part = jnp.sum(upstream * widened * inv_rms, axis=0)
    return (gradient.astype(jnp.bfloat16), gain_part)


def body(input_ids, target_ids, loss_mask, final_hidden, norm_gain, embed_cotangent, table):
    row_count = table.shape[0]
    embed_scale = math.sqrt(table.shape[1])
    owner = lax.axis_index(("dp", "vocab"))
    first_row = owner * row_count
    every_id, every_target, every_mask = (
        lax.all_gather(input_ids, "dp", axis=0, tiled=True),
        lax.all_gather(target_ids, "dp", axis=0, tiled=True),
        lax.all_gather(loss_mask, "dp", axis=0, tiled=True),
    )
    token_total = every_id.shape[0]
    per_group = token_total // lax.axis_size("dp")
    share_rows = token_total // lax.axis_size(("dp", "vocab"))
    widened = final_hidden.astype(jnp.float32)
    inv_rms = lax.rsqrt(jnp.mean(widened * widened, axis=1, keepdims=True) + EPSILON)
    normed = (widened * inv_rms * norm_gain).astype(jnp.bfloat16)
    normed_all, cotangent_all = (
        lax.all_gather(normed, "dp", axis=0, tiled=True),
        lax.all_gather(embed_cotangent, "dp", axis=0, tiled=True),
    )

    def lookup_term():
        wanted = lax.slice_in_dim(every_id, 0, per_group * lax.axis_size("dp"), axis=0) - first_row
        inside = (wanted >= 0) & (wanted < row_count)
        picked = jnp.take(table, jnp.clip(wanted, 0, row_count - 1), axis=0)
        return jnp.where(inside[:, None], picked.astype(jnp.float32), 0.0)

    group_rows = lax.psum_scatter(
        lookup_term().astype(jnp.bfloat16), "dp", scatter_dimension=0, tiled=True
    ).astype(jnp.float32)
    found = lax.psum(group_rows.astype(jnp.bfloat16), "vocab").astype(jnp.float32)
    embedded = (found * embed_scale).astype(jnp.bfloat16)
    raw_logits = lax.dot_general(
        normed_all, table, (((1,), (1,)), ((), ())), preferred_element_type=jnp.float32
    )
    capped = SOFTCAP * jnp.tanh(raw_logits / SOFTCAP)
    exp_logits = jnp.exp(capped)
    local_targets = every_target - first_row
    target_hit = lax.broadcasted_iota(jnp.int32, capped.shape, 1) == local_targets[:, None]
    token_weight = every_mask.astype(jnp.float32)
    picked_sum = jnp.sum(token_weight * jnp.sum(jnp.where(target_hit, capped, 0.0), axis=1))
    sum_exp, target_sum = lax.psum((jnp.sum(exp_logits, axis=1), picked_sum), ("dp", "vocab"))
    loss = (jnp.sum(token_weight * jnp.log(sum_exp)) - target_sum) / jnp.maximum(
        jnp.sum(token_weight), 1.0
    )
    slope = (
        token_weight[:, None]
        * (exp_logits / sum_exp[:, None] - target_hit.astype(jnp.float32))
        * (1.0 - (capped / SOFTCAP) ** 2)
    )
    slope_low = slope.astype(jnp.bfloat16)
    head_part = lax.dot_general(
        slope_low, normed_all, (((0,), (0,)), ((), ())), preferred_element_type=jnp.float32
    )
    local_ids = every_id - first_row
    owned = (local_ids >= 0) & (local_ids < row_count)
    segment_ids = jnp.where(owned, local_ids, row_count)
    embed_part = (
        jax.ops.segment_sum(
            cotangent_all.astype(jnp.float32), segment_ids, num_segments=row_count + 1
        )[:row_count]
        * embed_scale
    )
    table_grad = (head_part + embed_part).astype(jnp.bfloat16)

    def upstream_term():
        block = lax.slice_in_dim(slope_low, 0, share_rows * lax.axis_size(("dp", "vocab")), axis=0)
        return jnp.dot(block, table, preferred_element_type=jnp.float32)

    upstream = lax.psum_scatter(upstream_term(), ("dp", "vocab"), scatter_dimension=0, tiled=True)
    offset_rows = lax.axis_index("vocab") * share_rows
    widened_share = lax.dynamic_slice_in_dim(widened, offset_rows, share_rows, 0)
    inv_share = lax.dynamic_slice_in_dim(inv_rms, offset_rows, share_rows, 0)
    gradient_share, gain_part = norm_backward(upstream, widened_share, inv_share, norm_gain)
    gain_grad = lax.psum(gain_part, ("dp", "vocab"))
    grad_hidden = lax.all_gather(gradient_share, "vocab", axis=0, tiled=True)
    return (embedded, loss, grad_hidden, gain_grad, table_grad)


def solution(mesh):
    placed = (
        P("dp"),
        P("dp"),
        P("dp"),
        P("dp", None),
        P(),
        P("dp", None),
        P(("dp", "vocab"), None),
    )
    return jax.shard_map(
        body,
        mesh=mesh,
        in_specs=placed,
        out_specs=(P("dp", None), P(), P("dp", None), P(), P(("dp", "vocab"), None)),
        check_vma=False,
    )
```

profile of v0, /device:TPU:0, one launch (start us, length us, event | category | flops | bytes accessed | tf_op | source)
XLA Modules:
  0.0 414.2 jit_solution(4255250760945379497)
XLA Ops:
  7.2 0.0 reduce-scatter.2.cloned.1.call-start
  7.2 1.9 multiply_reduce_fusion
  9.2 0.7 broadcast_subtract_fusion
  9.9 0.0 copy-start.4
  9.9 8.1 %select_reduce_fusion = (f32[256]{0:T(256)S(1)}, f32[256]{0:T(256)S(1)}, f32[256,2000]{0,1:T(8,128)S(1)}) fusion(s32[256]{0:T(256)S(1)} %broadcast_subtract_fusion, bf16[2000,3584]{1,0:T(8,128)(2,1)} %param.13, f32[3584]{0:T(1024)} %param.11, f32[256]{0:T(256)S(1)} %add_rsqrt_fusion, bf16[256,3584]{1,0:T(8,128)(2,1)} %param.10), kind=kOutput, calls=%fused_computation.15 | convolution fusion | flops 3676757504 | bytes 18237440 | tf_op jit(solution)/shard_map/dot_general | solution.py:51
  18.0 0.0 copy-start.1
  18.0 42.0 %psum.29 = f32[256]{0:T(256)S(1)} all-reduce(f32[256]{0:T(256)S(1)} %get-tuple-element.8), channel_id=1, replica_groups=mesh['dp'=1,'vocab'=32] {'dp','vocab'}, use_global_device_ids=true, to_apply=%region_3.4 | all-reduce | flops 256 | bytes 2048 | tf_op jit(solution)/shard_map/psum | solution.py:60
  60.0 0.0 copy-done.4
  60.0 9.4 %fusion.7 = f32[256,3584]{1,0:T(8,128)} fusion(bf16[2000,3584]{1,0:T(8,128)(2,1)} %param.13, f32[256,2000]{0,1:T(8,128)S(1)} %get-tuple-element.19, f32[256]{0:T(256)S(1)} %psum.29, f32[256]{0:T(256)S(1)} %convert_element_type.42, s32[256]{0:T(256)S(1)} %broadcast_subtract_fusion), kind=kOutput, calls=%fused_computation.34 | convolution fusion | flops 3675136000 | bytes 20057088 | tf_op jit(solution)/shard_map/dot_general | solution.py:86
  69.3 0.0 copy-done.1
  69.3 0.0 copy-start.3
  69.3 0.0 reduce-scatter.2.cloned.1.call-update
  69.4 0.0 all-reduce.3.cloned.1.call-start
  69.4 0.6 copy-done.3
  70.0 11.7 %gather_fusion = bf16[256,3584]{1,0:T(8,128)(2,1)} fusion(bf16[2000,3584]{1,0:T(8,128)(2,1)} %param.13, s32[1024]{0:T(1024)S(1)} %pad_clamp_fusion), kind=kCustom, calls=%fused_computation | custom fusion | bytes 3671040 | tf_op jit(solution)/shard_map/jit(_take)/gather | solution.py:43
  81.7 0.0 copy-start
  81.7 3.9 select_convert_fusion
  85.6 0.0 all-reduce.3.cloned.1.call-update
  85.6 0.0 copy-start.2
  85.6 0.2 all-gather.2.cloned.1.call-start
  85.9 0.0 copy-done
  85.9 2.2 convert_element_type.43
  88.1 0.1 fusion.6
  88.2 0.6 convert_reduce_fusion
  89.5 121.3 %reduce-scatter.2.cloned.1.call-done = f32[8,3584]{1,0:T(8,128)} async-done(((f32[256,3584]{1,0:T(8,128)}), f32[8,3584]{1,0:T(8,128)}) %reduce-scatter.2.cloned.1.call-update) | async-done | bytes 114704 | tf_op jit(solution)/shard_map/reduce_scatter | solution.py:88
  210.7 0.0 copy-done.2
  210.7 1.2 multiply_reduce_fusion.1
  211.9 1.7 subtract_convert_fusion
  213.6 0.0 all-gather.2.cloned.1.call-update
  213.6 18.1 %scatter_custom_fusion = f32[2001,3584]{1,0:T(8,128)} fusion(s32[256]{0:T(256)S(1)} %subtract_select_fusion, f32[]{:T(128)} %constant.21.clone.1, bf16[256,3584]{1,0:T(8,128)(2,1)} %param.12), kind=kCustom, calls=%fused_computation.5 | custom fusion | flops 1835008 | bytes 30521348 | tf_op jit(solution)/shard_map/scatter-add | solution.py:77
  231.7 17.1 %fusion.1 = bf16[2000,3584]{1,0:T(8,128)(2,1)} fusion(f32[2001,3584]{1,0:T(8,128)} %scatter_custom_fusion, f32[3584]{0:T(1024)S(1)} %copy-done.2, f32[256]{0:T(256)S(1)} %add_rsqrt_fusion, bf16[256,3584]{1,0:T(8,128)(2,1)S(1)} %copy-done, f32[256,2000]{0,1:T(8,128)} %copy-done.1, f32[256]{0:T(256)S(1)} %psum.29, f32[256]{0:T(256)S(1)} %convert_element_type.42, ...), kind=kOutput, calls=%fused_computation.4 | convolution fusion | flops 3700310016 | bytes 46909440 | tf_op jit(solution)/shard_map/dot_general | solution.py:70
  248.8 97.3 %all-reduce.3.cloned.1.call-done = bf16[256,3584]{1,0:T(8,128)(2,1)} async-done(((bf16[256,3584]{1,0:T(8,128)(2,1)}), bf16[256,3584]{1,0:T(8,128)(2,1)}) %all-reduce.3.cloned.1.call-update) | async-done | bytes 1835024 | tf_op jit(solution)/shard_map/psum | solution.py:49
  346.2 3.0 multiply_convert_fusion.1
  349.2 39.6 %all-reduce = (f32[]{:T(128)}, f32[3584]{0:T(1024)}) all-reduce(f32[]{:T(128)} %get-tuple-element.11, f32[3584]{0:T(1024)S(1)} %get-tuple-element.5), channel_id=1, replica_groups=mesh['dp'=1,'vocab'=32] {'dp','vocab'}, use_global_device_ids=true, to_apply=%region_7.8 | all-reduce | flops 3585 | bytes 28680 | tf_op jit(solution)/shard_map/psum | solution.py:60
  390.1 13.7 %all-gather.2.cloned.1.call-done = bf16[256,3584]{1,0:T(8,128)(2,1)} async-done(((bf16[8,3584]{1,0:T(8,128)(2,1)}), bf16[256,3584]{1,0:T(8,128)(2,1)}) %all-gather.2.cloned.1.call-update) | async-done | bytes 1835024 | tf_op jit(solution)/shard_map/all_gather | solution.py:94
  403.7 2.8 copy.14
  (6 shorter events, 0.0 us)
Async XLA Ops:
  7.2 203.6 %reduce-scatter.2.cloned.1.call-start = ((), (), s32[]{:S(2)}) async-start(), calls=%async_computation.2 | async-start | bytes 3784704 | tf_op jit(solution)/shard_map/reduce_scatter | solution.py:88
  9.9 50.1 %copy-start.4 = (s32[256]{0:T(256)S(1)}, s32[256]{0:T(256)}, u32[]{:S(2)}) copy-start(s32[256]{0:T(256)} %param.9) | copy-start | bytes 3076
  18.0 51.4 %copy-start.1 = (f32[256,2000]{0,1:T(8,128)}, f32[256,2000]{0,1:T(8,128)S(1)}, u32[]{:S(2)}) copy-start(f32[256,2000]{0,1:T(8,128)S(1)} %get-tuple-element.19) | copy-start | bytes 6144004
  69.3 0.7 copy-start.3
  69.4 276.8 %all-reduce.3.cloned.1.call-start = ((), (), s32[]{:S(2)}) async-start(), calls=%async_computation.1 | async-start | bytes 3670016 | tf_op jit(solution)/shard_map/psum | solution.py:49
  81.7 4.1 copy-start
  85.6 125.1 %copy-start.2 = (f32[3584]{0:T(1024)S(1)}, f32[3584]{0:T(1024)}, u32[]{:S(2)}) copy-start(f32[3584]{0:T(1024)} %param.11) | copy-start | bytes 43012
  85.6 318.1 %all-gather.2.cloned.1.call-start = ((), (), s32[]{:S(2)}) async-start(), calls=%async_computation.3 | async-start | bytes 1892352 | tf_op jit(solution)/shard_map/all_gather | solution.py:94
Sparse Core Ops, SparseCore 0:
  69.5 141.1 reduce-scatter.1
  216.6 129.4 all-reduce.2
  349.0 54.6 all-gather.1
where the time goes:
time: 415 us; the launch traced here: 414 us
  waiting for transfers between devices  232 us (56%)
  blocking collectives  81.6 us (20%)
  matrix products  34.6 us (8%)
  other arithmetic  33.4 us (8%)
  between operations  16.9 us (4%)
  local copies, waits for them, and re-layouts  15.1 us (4%)
    reduce_scatter x1, waiting for transfers between devices, body(): lax.psum_scatter(upstream_term(), ('dp', 'vocab'), scatter_dimension=0, t...  121 us
    psum x1, waiting for transfers between devices, body(): lax.psum(group_rows.astype(jnp.bfloat16), 'vocab').astype(jnp.float32)  97.3 us
    psum x2, blocking collectives, body(): lax.psum((jnp.sum(exp_logits, axis=1), picked_sum), ('dp', 'vocab'))  81.6 us
    scatter-add x1, other arithmetic, body(): jax.ops.segment_sum(cotangent_all.astype(jnp.float32), segment_ids, num_s...  18.1 us
    dot_general x1, matrix products, body(): lax.dot_general(slope_low, normed_all, (((0,), (0,)), ((), ())), preferre...  17.1 us
    all_gather x1, waiting for transfers between devices, body(): grad_hidden = lax.all_gather(gradient_share, 'vocab', axis=0, tiled=True)  13.7 us
    gather x1, local copies, waits for them, and re-layouts, lookup_term(): picked = jnp.take(table, jnp.clip(wanted, 0, row_count - 1), axis=0)  11.7 us
    dot_general x1, matrix products, upstream_term(): return jnp.dot(block, table, preferred_element_type=jnp.float32)  9.38 us
  transfers between devices with their start and end apart: 3, of which 3 were waited for; matrix products, arithmetic and copies ran while one was open for 14% of the time, Pallas kernels for 0%

commit v1 on v0

--- a/solution.py
+++ b/solution.py
@@ -57,7 +57,9 @@
     target_hit = lax.broadcasted_iota(jnp.int32, capped.shape, 1) == local_targets[:, None]
     token_weight = every_mask.astype(jnp.float32)
     picked_sum = jnp.sum(token_weight * jnp.sum(jnp.where(target_hit, capped, 0.0), axis=1))
-    sum_exp, target_sum = lax.psum((jnp.sum(exp_logits, axis=1), picked_sum), ("dp", "vocab"))
+    sum_exp, target_sum = lax.psum(
+        lax.psum((jnp.sum(exp_logits, axis=1), picked_sum), "vocab"), "dp"
+    )
     loss = (jnp.sum(token_weight * jnp.log(sum_exp)) - target_sum) / jnp.maximum(
         jnp.sum(token_weight), 1.0
     )

time: 415 us -> 415 us (level)
  no operation moved by 1% of the time
where the time goes in v1:
time: 415 us; the launch traced here: 414 us
  waiting for transfers between devices  232 us (56%)
  blocking collectives  81.6 us (20%)
  matrix products  34.6 us (8%)
  other arithmetic  33.4 us (8%)
  between operations  16.9 us (4%)
  local copies, waits for them, and re-layouts  15.1 us (4%)
    reduce_scatter x1, waiting for transfers between devices, body(): lax.psum_scatter(upstream_term(), ('dp', 'vocab'), scatter_dimension=0, t...  121 us
    psum x1, waiting for transfers between devices, body(): lax.psum(group_rows.astype(jnp.bfloat16), 'vocab').astype(jnp.float32)  97.3 us
    psum x2, blocking collectives, body(): lax.psum((jnp.sum(exp_logits, axis=1), picked_sum), 'vocab')  81.6 us
    scatter-add x1, other arithmetic, body(): jax.ops.segment_sum(cotangent_all.astype(jnp.float32), segment_ids, num_s...  18.1 us
    dot_general x1, matrix products, body(): lax.dot_general(slope_low, normed_all, (((0,), (0,)), ((), ())), preferre...  17.1 us
    all_gather x1, waiting for transfers between devices, body(): grad_hidden = lax.all_gather(gradient_share, 'vocab', axis=0, tiled=True)  13.7 us
    gather x1, local copies, waits for them, and re-layouts, lookup_term(): picked = jnp.take(table, jnp.clip(wanted, 0, row_count - 1), axis=0)  11.7 us
    dot_general x1, matrix products, upstream_term(): return jnp.dot(block, table, preferred_element_type=jnp.float32)  9.38 us
  transfers between devices with their start and end apart: 3, of which 3 were waited for; matrix products, arithmetic and copies ran while one was open for 14% of the time, Pallas kernels for 0%

profile of v1, /device:TPU:0, one launch (start us, length us, event | category | flops | bytes accessed | tf_op | source)
XLA Modules:
  0.0 414.2 jit_solution(4255250760945379497)
XLA Ops:
  7.2 0.0 reduce-scatter.2.cloned.1.call-start
  7.2 1.9 multiply_reduce_fusion
  9.2 0.7 broadcast_subtract_fusion
  9.9 0.0 copy-start.4
  9.9 8.1 %select_reduce_fusion = (f32[256]{0:T(256)S(1)}, f32[256]{0:T(256)S(1)}, f32[256,2000]{0,1:T(8,128)S(1)}) fusion(s32[256]{0:T(256)S(1)} %broadcast_subtract_fusion, bf16[2000,3584]{1,0:T(8,128)(2,1)} %param.13, f32[3584]{0:T(1024)} %param.11, f32[256]{0:T(256)S(1)} %add_rsqrt_fusion, bf16[256,3584]{1,0:T(8,128)(2,1)} %param.10), kind=kOutput, calls=%fused_computation.15 | convolution fusion | flops 3676757504 | bytes 18237440 | tf_op jit(solution)/shard_map/dot_general | solution.py:51
  18.0 0.0 copy-start.1
  18.0 42.0 %psum.29 = f32[256]{0:T(256)S(1)} all-reduce(f32[256]{0:T(256)S(1)} %get-tuple-element.8), channel_id=1, replica_groups=mesh['dp'=1,'vocab'=32] {'vocab'}, use_global_device_ids=true, to_apply=%region_3.4 | all-reduce | flops 256 | bytes 2048 | tf_op jit(solution)/shard_map/psum | solution.py:61
  60.0 0.0 copy-done.4
  60.0 9.4 %fusion.7 = f32[256,3584]{1,0:T(8,128)} fusion(bf16[2000,3584]{1,0:T(8,128)(2,1)} %param.13, f32[256,2000]{0,1:T(8,128)S(1)} %get-tuple-element.19, f32[256]{0:T(256)S(1)} %psum.29, f32[256]{0:T(256)S(1)} %convert_element_type.42, s32[256]{0:T(256)S(1)} %broadcast_subtract_fusion), kind=kOutput, calls=%fused_computation.34 | convolution fusion | flops 3675136000 | bytes 20057088 | tf_op jit(solution)/shard_map/dot_general | solution.py:88
  69.3 0.0 copy-done.1
  69.3 0.0 copy-start.3
  69.3 0.0 reduce-scatter.2.cloned.1.call-update
  69.4 0.0 all-reduce.3.cloned.1.call-start
  69.4 0.6 copy-done.3
  70.0 11.7 %gather_fusion = bf16[256,3584]{1,0:T(8,128)(2,1)} fusion(bf16[2000,3584]{1,0:T(8,128)(2,1)} %param.13, s32[1024]{0:T(1024)S(1)} %pad_clamp_fusion), kind=kCustom, calls=%fused_computation | custom fusion | bytes 3671040 | tf_op jit(solution)/shard_map/jit(_take)/gather | solution.py:43
  81.7 0.0 copy-start
  81.7 3.9 select_convert_fusion
  85.6 0.0 all-reduce.3.cloned.1.call-update
  85.6 0.0 copy-start.2
  85.6 0.2 all-gather.2.cloned.1.call-start
  85.9 0.0 copy-done
  85.9 2.2 convert_element_type.43
  88.1 0.1 fusion.6
  88.2 0.6 convert_reduce_fusion
  89.5 121.3 %reduce-scatter.2.cloned.1.call-done = f32[8,3584]{1,0:T(8,128)} async-done(((f32[256,3584]{1,0:T(8,128)}), f32[8,3584]{1,0:T(8,128)}) %reduce-scatter.2.cloned.1.call-update) | async-done | bytes 114704 | tf_op jit(solution)/shard_map/reduce_scatter | solution.py:90
  210.7 0.0 copy-done.2
  210.7 1.2 multiply_reduce_fusion.1
  211.9 1.7 subtract_convert_fusion
  213.6 0.0 all-gather.2.cloned.1.call-update
  213.6 18.1 %scatter_custom_fusion = f32[2001,3584]{1,0:T(8,128)} fusion(s32[256]{0:T(256)S(1)} %subtract_select_fusion, f32[]{:T(128)} %constant.21.clone.1, bf16[256,3584]{1,0:T(8,128)(2,1)} %param.12), kind=kCustom, calls=%fused_computation.5 | custom fusion | flops 1835008 | bytes 30521348 | tf_op jit(solution)/shard_map/scatter-add | solution.py:79
  231.7 17.1 %fusion.1 = bf16[2000,3584]{1,0:T(8,128)(2,1)} fusion(f32[2001,3584]{1,0:T(8,128)} %scatter_custom_fusion, f32[3584]{0:T(1024)S(1)} %copy-done.2, f32[256]{0:T(256)S(1)} %add_rsqrt_fusion, bf16[256,3584]{1,0:T(8,128)(2,1)S(1)} %copy-done, f32[256,2000]{0,1:T(8,128)} %copy-done.1, f32[256]{0:T(256)S(1)} %psum.29, f32[256]{0:T(256)S(1)} %convert_element_type.42, ...), kind=kOutput, calls=%fused_computation.4 | convolution fusion | flops 3700310016 | bytes 46909440 | tf_op jit(solution)/shard_map/dot_general | solution.py:72
  248.8 97.3 %all-reduce.3.cloned.1.call-done = bf16[256,3584]{1,0:T(8,128)(2,1)} async-done(((bf16[256,3584]{1,0:T(8,128)(2,1)}), bf16[256,3584]{1,0:T(8,128)(2,1)}) %all-reduce.3.cloned.1.call-update) | async-done | bytes 1835024 | tf_op jit(solution)/shard_map/psum | solution.py:49
  346.2 3.0 multiply_convert_fusion.1
  349.2 39.6 %all-reduce = (f32[]{:T(128)}, f32[3584]{0:T(1024)}) all-reduce(f32[]{:T(128)} %get-tuple-element.11, f32[3584]{0:T(1024)S(1)} %get-tuple-element.5), channel_id=1, replica_groups=mesh['dp'=1,'vocab'=32] {'vocab'}, use_global_device_ids=true, to_apply=%region_7.8 | all-reduce | flops 3585 | bytes 28680 | tf_op jit(solution)/shard_map/psum | solution.py:61
  390.1 13.7 %all-gather.2.cloned.1.call-done = bf16[256,3584]{1,0:T(8,128)(2,1)} async-done(((bf16[8,3584]{1,0:T(8,128)(2,1)}), bf16[256,3584]{1,0:T(8,128)(2,1)}) %all-gather.2.cloned.1.call-update) | async-done | bytes 1835024 | tf_op jit(solution)/shard_map/all_gather | solution.py:96
  403.7 2.8 copy.14
  (6 shorter events, 0.0 us)
Async XLA Ops:
  7.2 203.6 %reduce-scatter.2.cloned.1.call-start = ((), (), s32[]{:S(2)}) async-start(), calls=%async_computation.2 | async-start | bytes 3784704 | tf_op jit(solution)/shard_map/reduce_scatter | solution.py:90
  9.9 50.1 %copy-start.4 = (s32[256]{0:T(256)S(1)}, s32[256]{0:T(256)}, u32[]{:S(2)}) copy-start(s32[256]{0:T(256)} %param.9) | copy-start | bytes 3076
  18.0 51.4 %copy-start.1 = (f32[256,2000]{0,1:T(8,128)}, f32[256,2000]{0,1:T(8,128)S(1)}, u32[]{:S(2)}) copy-start(f32[256,2000]{0,1:T(8,128)S(1)} %get-tuple-element.19) | copy-start | bytes 6144004
  69.3 0.7 copy-start.3
  69.4 276.8 %all-reduce.3.cloned.1.call-start = ((), (), s32[]{:S(2)}) async-start(), calls=%async_computation.1 | async-start | bytes 3670016 | tf_op jit(solution)/shard_map/psum | solution.py:49
  81.7 4.1 copy-start
  85.6 125.1 %copy-start.2 = (f32[3584]{0:T(1024)S(1)}, f32[3584]{0:T(1024)}, u32[]{:S(2)}) copy-start(f32[3584]{0:T(1024)} %param.11) | copy-start | bytes 43012
  85.6 318.1 %all-gather.2.cloned.1.call-start = ((), (), s32[]{:S(2)}) async-start(), calls=%async_computation.3 | async-start | bytes 1892352 | tf_op jit(solution)/shard_map/all_gather | solution.py:96
Sparse Core Ops, SparseCore 0:
  69.5 141.1 reduce-scatter.1
  216.6 129.4 all-reduce.2
  349.0 54.6 all-gather.1
